TPU v7x, 32 devices: a whole 2x2x4 slice. The times are simulated.
32 devices in a mesh: seq: 8 (over y, x, core), head: 4 (over z).
Axes of the slice: x: 2, y: 2, z: 4, core: 2. Of those that a mesh axis runs over, the one named last changes fastest.
Arguments:
- mid: bfloat16 [2048, 3072], P('seq'), may hold values from -20 to 20
- second_in: bfloat16 [2048, 3072], P('seq'), may hold values from -20 to 20
- cotangent: bfloat16 [2048, 3072], P('seq'), may hold values from -6 to 6
- w_key: bfloat16 [3072, 1024], P(None, 'head'), may hold values from -0.109375 to 0.109375
- w_value: bfloat16 [3072, 1024], P(None, 'head'), may hold values from -0.109375 to 0.109375
- w_query: bfloat16 [2, 3072, 3072], P(None, None, 'head'), may hold values from -0.109375 to 0.109375
- w_out: bfloat16 [2, 3072, 3072], P(None, 'head'), may hold values from -0.109375 to 0.109375
- w_ret_out: bfloat16 [3072, 3072], P('head'), may hold values from -0.109375 to 0.109375
- ret_query: bfloat16 [2048, 3072], P('seq', 'head'), may hold values from -6 to 6
- ret_key: bfloat16 [2048, 3072], P('seq', 'head'), may hold values from -3 to 3
- ret_value: bfloat16 [2048, 3072], P('seq', 'head'), may hold values from -6 to 6
- gate: float32 [24, 2048], P('head', 'seq'), may hold values from 0 to 6
- decay_exp: int32 [24], P('head'), may hold values from 0 to 256
- mask_start: int32 [16], P('seq'), may hold values from 0 to 1920, as said below
Outputs:
- grad_mid: bfloat16 [2048, 3072], P('seq')
- grad_ret_query: bfloat16 [2048, 3072], P('seq', 'head')
- grad_ret_key: bfloat16 [2048, 3072], P('seq', 'head')
- grad_ret_value: bfloat16 [2048, 3072], P('seq', 'head')
- grad_w_key: float32 [3072, 1024], P(None, 'head')
- grad_w_value: float32 [3072, 1024], P(None, 'head')
Inputs may be any that keep to these rules, and one draw needn't show every extreme that they name: `mask_start`: the entry of each block of 128 queries is at most the position of that block's first query.
All inputs are finite; a program needn't handle non-finite values.
Results may differ from a plain program's by a relative error of at most 0.025.
The roundings to bfloat16 on the way count: a program that leaves them out, or rounds other values in their place, can miss the bound.
Values may be sent and summed in bfloat16 or wider, within the bound.
A program may use at most 192 MiB of HBM per device.

v0:
```python
import math
import jax
import jax.numpy as jnp
from jax import lax
from jax.sharding import PartitionSpec as P

E = 128
BLK = 128
RC = 128


def carried_in(value, axis, combine, identity, reverse):
    peers, position = (lax.axis_size(axis), lax.axis_index(axis))
    everything = jax.tree.map(lambda part: lax.all_gather(part, axis), value)
    start = jax.tree.map(
        lambda part, zero: jnp.broadcast_to(jnp.asarray(zero, part.dtype), part.shape),
        value,
        identity,
    )

    def lap(k, before):
        at = peers - 1 - k if reverse else k
        reached = at > position if reverse else at < position
        new = combine(before, jax.tree.map(lambda part: part[at], everything))
        return jax.tree.map(lambda a, b: jnp.where(reached, a, b), new, before)

    return lax.fori_loop(0, peers, lap, start)


def contract_last(left, right):
    return lax.dot_general(
        left, right, (((1,), (1,)), ((), ())), preferred_element_type=jnp.float32
    )


def attend_back(layer_in, w_query_l, w_out_l, upstream, keys, values, visible):
    row_count = layer_in.shape[0]
    key_count = keys.shape[0]
    kv_heads = keys.shape[1] // E
    factor = 1.0 / math.sqrt(E)
    queries = jnp.dot(layer_in, w_query_l, preferred_element_type=jnp.float32).astype(jnp.bfloat16)
    group = queries.shape[1] // keys.shape[1]
    grad_out = contract_last(upstream, w_out_l).astype(jnp.bfloat16)
    query_heads = queries.reshape(row_count, kv_heads, group, E)
    grad_heads = grad_out.reshape(row_count, kv_heads, group, E)
    key_heads = keys.reshape(key_count, kv_heads, E)
    value_heads = values.reshape(key_count, kv_heads, E)
    scores = (
        jnp.einsum("tkge,ske->kgts", query_heads, key_heads, preferred_element_type=jnp.float32)
        * factor
    )
    scores = jnp.where(visible, scores, -jnp.inf)
    top = jnp.max(scores, axis=-1, keepdims=True)
    raised = jnp.exp(scores - top)
    probs = raised / jnp.sum(raised, axis=-1, keepdims=True)
    rounded = probs.astype(jnp.bfloat16)
    outputs = jnp.einsum(
        "kgts,ske->tkge", rounded, value_heads, preferred_element_type=jnp.float32
    ).astype(jnp.bfloat16)
    delta = jnp.sum(grad_heads.astype(jnp.float32) * outputs.astype(jnp.float32), axis=-1)
    delta = jnp.transpose(delta, (1, 2, 0))[..., None]
    dprobs = jnp.einsum(
        "tkge,ske->kgts", grad_heads, value_heads, preferred_element_type=jnp.float32
    )
    dscores = (probs * (dprobs - delta) * factor).astype(jnp.bfloat16)
    query_grad = jnp.einsum(
        "kgts,ske->tkge", dscores, key_heads, preferred_element_type=jnp.float32
    )
    query_grad = query_grad.astype(jnp.bfloat16).reshape(row_count, -1)
    key_part = jnp.einsum(
        "kgts,tkge->ske", dscores, query_heads, preferred_element_type=jnp.float32
    ).reshape(key_count, -1)
    value_part = jnp.einsum(
        "kgts,tkge->ske", rounded, grad_heads, preferred_element_type=jnp.float32
    ).reshape(key_count, -1)
    return (contract_last(query_grad, w_query_l), key_part, value_part)


def retention_states(ret_key, ret_value, gate, decay_exp):
    length, width = ret_key.shape
    heads = gate.shape[0]
    size = width // heads
    count = length // RC
    key_blocks = ret_key.reshape(count, RC, heads, size)
    value_blocks = ret_value.reshape(count, RC, heads, size)
    rate = jnp.exp2(-decay_exp.astype(jnp.float32) / 64.0)
    accum = jnp.cumsum((-rate[:, None] * gate).reshape(heads, count, RC), axis=2)
    ends = accum[:, :, -1]
    shrink = jnp.transpose(jnp.exp(ends[:, :, None] - accum), (1, 2, 0))[..., None]
    weighted = (shrink * key_blocks).astype(jnp.bfloat16)
    own_state = jnp.einsum(
        "csha,cshb->hcab", weighted, value_blocks, preferred_element_type=jnp.float32
    )
    return (accum, ends, shrink, own_state)


def grad_states(ret_query, grad_o, accum):
    heads, count, block = accum.shape
    size = ret_query.shape[1] // heads
    query_blocks = ret_query.reshape(count, block, heads, size)
    grad_blocks = grad_o.reshape(count, block, heads, size)
    grow = jnp.transpose(jnp.exp(accum), (1, 2, 0))[..., None]
    weighted = (grow * query_blocks).astype(jnp.bfloat16)
    own_grad = (
        jnp.einsum("ctha,cthb->hcab", weighted, grad_blocks, preferred_element_type=jnp.float32) / E
    )
    return (grow, own_grad)


def retention_grads(ret_query, ret_key, ret_value, grad_o, accum, shrink, grow, entering, after):
    length, width = ret_query.shape
    heads, count, block = accum.shape
    size = width // heads
    shape4 = (count, block, heads, size)
    query_blocks = ret_query.reshape(shape4)
    key_blocks = ret_key.reshape(shape4)
    value_blocks = ret_value.reshape(shape4)
    grad_blocks = grad_o.reshape(shape4)
    lower = jnp.arange(block)[:, None] >= jnp.arange(block)[None, :]
    diff = accum[:, :, :, None] - accum[:, :, None, :]
    weights = jnp.where(lower, jnp.exp(jnp.where(lower, diff, 0.0)), 0.0)
    first = (
        weights
        * jnp.einsum(
            "ctha,csha->hcts", grad_blocks, value_blocks, preferred_element_type=jnp.float32
        )
    ).astype(jnp.bfloat16)
    second = (
        weights
        * jnp.einsum(
            "ctha,csha->hcts", query_blocks, key_blocks, preferred_element_type=jnp.float32
        )
    ).astype(jnp.bfloat16)
    inner_query = jnp.einsum(
        "hcts,csha->ctha", first, key_blocks, preferred_element_type=jnp.float32
    )
    inner_key = jnp.einsum(
        "hcts,ctha->csha", first, query_blocks, preferred_element_type=jnp.float32
    )
    inner_value = jnp.einsum(
        "hcts,ctha->csha", second, grad_blocks, preferred_element_type=jnp.float32
    )
    highest = lax.Precision.HIGHEST
    carried_query = jnp.einsum(
        "cthb,hcab->ctha", grad_blocks.astype(jnp.float32), entering, precision=highest
    )
    carried_key = jnp.einsum(
        "cshb,hcab->csha", value_blocks.astype(jnp.float32), after, precision=highest
    )
    carried_value = jnp.einsum(
        "csha,hcab->cshb", key_blocks.astype(jnp.float32), after, precision=highest
    )
    grad_query = (
        ((inner_query + grow * carried_query) / E).astype(jnp.bfloat16).reshape(length, width)
    )
    grad_key = (inner_key / E + shrink * carried_key).astype(jnp.bfloat16).reshape(length, width)
    grad_value = (
        (inner_value / E + shrink * carried_value).astype(jnp.bfloat16).reshape(length, width)
    )
    return (grad_query, grad_key, grad_value)


def combine_forward(earlier, later):
    return (earlier[0] * later[0], later[0] * earlier[1] + later[1])


def combine_backward(earlier, later):
    return (earlier[0] * later[0], later[1] + later[0] * earlier[1])


def head_total(partial_value, residual):
    summed = lax.psum(partial_value, "head")
    return (residual.astype(jnp.float32) + summed).astype(jnp.bfloat16)


def reduce_keys(key_part, value_part):
    return (
        lax.psum_scatter(key_part, "seq", scatter_dimension=0, tiled=True),
        lax.psum_scatter(value_part, "seq", scatter_dimension=0, tiled=True),
    )


def local(
    mid,
    second_in,
    cotangent,
    w_key,
    w_value,
    w_query,
    w_out,
    w_ret_out,
    ret_query,
    ret_key,
    ret_value,
    gate,
    decay_exp,
    mask_start,
):
    row_count = mid.shape[0]
    accum, ends, shrink, own_state = retention_states(ret_key, ret_value, gate, decay_exp)
    decay_rows = jnp.exp(ends)
    count = decay_rows.shape[1]
    device_decay = jnp.prod(decay_rows, axis=1)[:, None, None]
    device_state = jnp.zeros_like(own_state[:, 0])
    for block in range(count):
        device_state = decay_rows[:, block, None, None] * device_state + own_state[:, block]
    decay_before, incoming = carried_in(
        (device_decay, device_state),
        "seq",
        combine_forward,
        (jnp.ones_like(device_decay), jnp.zeros_like(device_state)),
        False,
    )
    keys_own = jnp.dot(mid, w_key, preferred_element_type=jnp.float32).astype(jnp.bfloat16)
    values_own = jnp.dot(mid, w_value, preferred_element_type=jnp.float32).astype(jnp.bfloat16)
    all_keys, all_values = (
        lax.all_gather(keys_own, "seq", axis=0, tiled=True),
        lax.all_gather(values_own, "seq", axis=0, tiled=True),
    )
    key_count = all_keys.shape[0]
    positions = lax.axis_index("seq") * row_count + jnp.arange(row_count, dtype=jnp.int32)
    first_seen = jnp.repeat(mask_start, BLK)
    key_positions = jnp.arange(key_count, dtype=jnp.int32)
    visible = (key_positions[None, :] >= first_seen[:, None]) & (
        key_positions[None, :] <= positions[:, None]
    )
    upper_in, upper_key, upper_value = attend_back(
        second_in, w_query[1], w_out[1], cotangent, all_keys, all_values, visible
    )
    upper_sums = reduce_keys(upper_key, upper_value)
    upstream = head_total(upper_in, cotangent)
    lower_in, lower_key, lower_value = attend_back(
        mid, w_query[0], w_out[0], upstream, all_keys, all_values, visible
    )
    lower_sums = reduce_keys(lower_key, lower_value)
    key_total = upper_sums[0] + lower_sums[0]
    value_total = upper_sums[1] + lower_sums[1]
    key_grad = key_total.astype(jnp.bfloat16)
    value_grad = value_total.astype(jnp.bfloat16)
    mid_part = lower_in + contract_last(key_grad, w_key) + contract_last(value_grad, w_value)
    grad_mid = head_total(mid_part, upstream)
    tokens_dims = (((0,), (0,)), ((), ()))
    key_weight_part = lax.dot_general(
        mid, key_grad, tokens_dims, preferred_element_type=jnp.float32
    )
    value_weight_part = lax.dot_general(
        mid, value_grad, tokens_dims, preferred_element_type=jnp.float32
    )
    grad_w_key, grad_w_value = lax.psum((key_weight_part, value_weight_part), "seq")
    grad_o = contract_last(grad_mid, w_ret_out).astype(jnp.bfloat16)
    grow, own_grad = grad_states(ret_query, grad_o, accum)
    device_grad = jnp.zeros_like(device_state)
    for block in reversed(range(count)):
        device_grad = own_grad[:, block] + decay_rows[:, block, None, None] * device_grad
    decay_after, outgoing = carried_in(
        (device_decay, device_grad),
        "seq",
        combine_backward,
        (jnp.ones_like(device_decay), jnp.zeros_like(device_grad)),
        True,
    )
    entering_list = []
    state_now = incoming
    for block in range(count):
        entering_list.append(state_now)
        state_now = decay_rows[:, block, None, None] * state_now + own_state[:, block]
    after_list = [state_now] * count
    state_now = outgoing
    for block in reversed(range(count)):
        after_list[block] = state_now
        state_now = own_grad[:, block] + decay_rows[:, block, None, None] * state_now
    entering = jnp.stack(entering_list, axis=1)
    after = jnp.stack(after_list, axis=1)
    grad_query, grad_key, grad_value = retention_grads(
        ret_query, ret_key, ret_value, grad_o, accum, shrink, grow, entering, after
    )
    return (grad_mid, grad_query, grad_key, grad_value, grad_w_key, grad_w_value)


def solution(mesh):
    placed = (
        P("seq", None),
        P("seq", None),
        P("seq", None),
        P(None, "head"),
        P(None, "head"),
        P(None, None, "head"),
        P(None, "head", None),
        P("head", None),
        P("seq", "head"),
        P("seq", "head"),
        P("seq", "head"),
        P("head", "seq"),
        P("head"),
        P("seq"),
    )
    return jax.shard_map(
        local,
        mesh=mesh,
        in_specs=placed,
        out_specs=(
            P("seq", None),
            P("seq", "head"),
            P("seq", "head"),
            P("seq", "head"),
            P(None, "head"),
            P(None, "head"),
        ),
        check_vma=False,
    )
```

profile of v0, /device:TPU:0, one launch (start us, length us, event | category | flops | bytes accessed | tf_op | source)
XLA Modules:
  0.0 662.4 jit_solution(6246297149138397294)
XLA Ops:
  19.3 4.6 fusion.62
  26.5 11.0 %all-gather.8.cloned.1.call-done = bf16[2048,256]{1,0:T(8,128)(2,1)} async-done(((bf16[256,256]{1,0:T(8,128)(2,1)}), bf16[2048,256]{1,0:T(8,128)(2,1)}) %all-gather.8.cloned.1.call-update) | async-done | bytes 1048592 | tf_op jit(solution)/shard_map/all_gather | solution.py:218
  42.6 20.8 %all-gather.6.cloned.1.call-done = bf16[2048,256]{1,0:T(8,128)(2,1)} async-done(((bf16[256,256]{1,0:T(8,128)(2,1)}), bf16[2048,256]{1,0:T(8,128)(2,1)}) %all-gather.6.cloned.1.call-update) | async-done | bytes 1048592 | tf_op jit(solution)/shard_map/all_gather | solution.py:217
  69.2 9.7 %fusion.133 = (f32[2,3,256]{2,1,0:T(4,128)S(1)}, f32[2,3,256,2048]{2,3,1,0:T(8,128)}) fusion(pred[256,2048]{0,1:T(8,128)(4,1)} %fusion.44, bf16[256,2,3,128]{0,3,2,1:T(8,128)(2,1)S(1)} %bitcast.325, bf16[2048,2,128,1]{2,1,0,3:T(2,128)(2,1)} %bitcast.312), kind=kOutput, calls=%fused_computation.176 | convolution fusion | flops 817891328 | bytes 14555136 | tf_op jit(solution)/shard_map/sub | solution.py:54
  79.0 8.2 %fusion.18 = bf16[2,3,256,2048]{2,3,1,0:T(8,128)(2,1)} fusion(f32[2,3,256,2048]{2,3,1,0:T(8,128)} %get-tuple-element.351, f32[2,3,256]{2,1,0:T(4,128)S(1)} %get-tuple-element.350), kind=kLoop, calls=%fused_computation.30 | loop fusion | flops 6291456 | bytes 18880512 | tf_op jit(solution)/shard_map/convert_element_type | solution.py:56
  91.1 5.8 fusion.9
  100.6 5.5 fusion.28
  112.0 9.9 %fusion.128 = (f32[2,3,256]{2,1,0:T(4,128)S(1)}, f32[2,3,256,2048]{2,3,1,0:T(8,128)}) fusion(pred[256,2048]{0,1:T(8,128)(4,1)} %fusion.44, bf16[256,2,3,128]{0,3,2,1:T(8,128)(2,1)S(1)} %bitcast.323, bf16[2048,2,128,1]{2,1,0,3:T(2,128)(2,1)} %bitcast.313), kind=kOutput, calls=%fused_computation.175 | convolution fusion | flops 817891328 | bytes 14555136 | tf_op jit(solution)/shard_map/sub | solution.py:54
  121.9 8.3 %fusion.19 = bf16[2,3,256,2048]{2,3,1,0:T(8,128)(2,1)} fusion(f32[2,3,256,2048]{2,3,1,0:T(8,128)} %get-tuple-element.349, f32[2,3,256]{2,1,0:T(4,128)S(1)} %get-tuple-element.348), kind=kLoop, calls=%fused_computation.31 | loop fusion | flops 6291456 | bytes 18880512 | tf_op jit(solution)/shard_map/convert_element_type | solution.py:56
  130.3 97.0 %all-reduce.6.cloned.1.call-done = f32[256,3072]{1,0:T(8,128)} async-done(((f32[256,3072]{1,0:T(8,128)}), f32[256,3072]{1,0:T(8,128)}) %all-reduce.6.cloned.1.call-update) | async-done | bytes 3145744 | tf_op jit(solution)/shard_map/psum | solution.py:172
  227.3 5.9 fusion.68
  238.4 5.9 fusion.6
  250.2 4.9 convolution_bitcast_fusion.2
  255.1 6.8 %fusion.43 = f32[2,128,2048]{2,1,0:T(8,128)} fusion(f32[2,128,2048]{2,1,0:T(8,128)S(1)} %convolution_bitcast_fusion.2, bf16[256,2,3,128]{0,3,2,1:T(8,128)(2,1)S(1)} %bitcast.319, bf16[2,3,256,2048]{2,3,1,0:T(8,128)(2,1)} %fusion.18), kind=kOutput, calls=%fused_computation.63 | convolution fusion | flops 805830656 | bytes 10878976 | tf_op jit(solution)/shard_map/kgts,tkge->ske/dot_general | solution.py:73
  265.8 5.6 fusion.22
  271.4 18.9 %reduce-scatter.3.cloned.1.call-done = f32[256,256]{0,1:T(8,128)} async-done(((f32[2048,256]{0,1:T(8,128)}), f32[256,256]{0,1:T(8,128)}) %reduce-scatter.3.cloned.1.call-update) | async-done | bytes 262160 | tf_op jit(solution)/shard_map/reduce_scatter | solution.py:178
  294.5 40.0 %reduce-scatter.5.cloned.1.call-done = f32[256,256]{0,1:T(8,128)} async-done(((f32[2048,256]{0,1:T(8,128)}), f32[256,256]{0,1:T(8,128)}) %reduce-scatter.5.cloned.1.call-update) | async-done | bytes 262160 | tf_op jit(solution)/shard_map/reduce_scatter | solution.py:179
  334.5 4.7 convolution_add_fusion
  354.9 105.6 %all-reduce.8.cloned.1.call-done = f32[256,3072]{1,0:T(8,128)} async-done(((f32[256,3072]{1,0:T(8,128)}), f32[256,3072]{1,0:T(8,128)}) %all-reduce.8.cloned.1.call-update) | async-done | bytes 3145744 | tf_op jit(solution)/shard_map/psum | solution.py:172
  477.0 14.7 %all-reduce = f32[48]{0:T(128)} all-reduce(f32[48]{0:T(128)} %dynamic-update-slice), channel_id=2, replica_groups=mesh['seq'=8,'head'=4] {'seq'}, use_global_device_ids=true, to_apply=%add | all-reduce | flops 48 | bytes 384
  496.0 18.2 %while.30 = (s32[]{:T(128)}, f32[6,128,128]{2,1,0:T(8,128)S(1)}, s32[]{:T(128)}, f32[8,6,1,1]{1,3,2,0:T(1,128)}, f32[8,6,128,128]{3,2,1,0:T(8,128)}, /*index=5*/s32[]{:T(128)}, s32[]{:T(128)}) while((s32[]{:T(128)}, f32[6,128,128]{2,1,0:T(8,128)S(1)}, s32[]{:T(128)}, f32[8,6,1,1]{1,3,2,0:T(1,128)}, ...), condition=%wide.region_15.16_spmd.clone, body=%wide.region_14.15_spmd.clone.sunk | while | flops 393220 | bytes 1179825 | solution.py:27
  516.0 86.0 %all-reduce.10.cloned.1.call-done = (f32[3072,256]{0,1:T(8,128)}, f32[3072,256]{0,1:T(8,128)}) async-done(((f32[3072,256]{0,1:T(8,128)}, f32[3072,256]{0,1:T(8,128)}), (f32[3072,256]{0,1:T(8,128)}, f32[3072,256]{0,1:T(8,128)})) %all-reduce.10.cloned.1.call-update) | async-done | bytes 6291472 | tf_op jit(solution)/shard_map/psum | solution.py:249
  614.2 22.0 %all-gather.12.cloned.1.call-done = f32[8,6,128,128]{3,2,1,0:T(8,128)} async-done(((f32[1,6,128,128]{3,2,1,0:T(8,128)}), f32[8,6,128,128]{3,2,1,0:T(8,128)}) %all-gather.12.cloned.1.call-update) | async-done | bytes 3145744 | tf_op jit(solution)/shard_map/all_gather | solution.py:14
  636.3 14.1 %while.31 = (s32[]{:T(128)}, f32[6,128,128]{2,1,0:T(8,128)S(1)}, s32[]{:T(128)}, f32[8,6,128,128]{3,2,1,0:T(8,128)}, f32[8,6,1,1]{1,3,2,0:T(1,128)}, /*index=5*/s32[]{:T(128)}, s32[]{:T(128)}, s32[]{:T(128)}, s32[]{:T(128)}) while((s32[]{:T(128)}, f32[6,128,128]{2,1,0:T(8,128)S(1)}, s32[]{:T(128)}, ...), condition=%wide.region_17.18_spmd.clone, body=%wide.region_16.17_spmd.clone.sunk | while | flops 393224 | bytes 1179887 | solution.py:27
  (209 shorter events, 144.6 us)
Async XLA Ops:
  7.2 30.4 %all-gather.8.cloned.1.call-start = ((), (), s32[]{:S(2)}) async-start(), calls=%async_computation.3 | async-start | bytes 1179648 | tf_op jit(solution)/shard_map/all_gather | solution.py:218
  11.2 52.2 %all-gather.6.cloned.1.call-start = ((), (), s32[]{:S(2)}) async-start(), calls=%async_computation.2 | async-start | bytes 1179648 | tf_op jit(solution)/shard_map/all_gather | solution.py:217
  13.9 213.3 %all-reduce.6.cloned.1.call-start = ((), (), s32[]{:S(2)}) async-start(), calls=%async_computation.4 | async-start | bytes 6291456 | tf_op jit(solution)/shard_map/psum | solution.py:172
  23.9 45.4 %copy-start.22 = (bf16[256,768]{0,1:T(8,128)(2,1)S(1)}, bf16[256,768]{0,1:T(8,128)(2,1)}, u32[]{:S(2)}) copy-start(bf16[256,768]{0,1:T(8,128)(2,1)} %copy.141) | copy-start | bytes 1179652
  91.0 8.5 %copy-start.3 = (bf16[2048,2,128,1]{0,2,3,1:T(8,128)(2,1)S(1)}, bf16[2048,2,128,1]{0,2,3,1:T(8,128)(2,1)}, u32[]{:S(2)}) copy-start(bf16[2048,2,128,1]{0,2,3,1:T(8,128)(2,1)} %copy.216) | copy-start | bytes 3145732
  106.1 184.2 %reduce-scatter.3.cloned.1.call-start = ((), (), s32[]{:S(2)}) async-start(), calls=%async_computation.8 | async-start | bytes 2359296 | tf_op jit(solution)/shard_map/reduce_scatter | solution.py:178
  112.0 9.9 %copy-start.11 = (bf16[256,768]{0,1:T(8,128)(2,1)}, bf16[256,768]{0,1:T(8,128)(2,1)S(1)}, u32[]{:S(2)}) copy-start(bf16[256,768]{0,1:T(8,128)(2,1)S(1)} %copy.151) | copy-start | bytes 1179652
  234.4 12.0 %slice-start = ((s8[6291456]{0:T(1024)(128)(4,1)}), s8[4194304]{0:T(1024)(128)(4,1)S(1)}, s32[]{:S(2)}) async-start(s8[6291456]{0:T(1024)(128)(4,1)} %bitcast.301), calls=%async_computation.11 | async-start | bytes 8388608
  238.4 8.1 %slice-start.1 = ((s8[6291456]{0:T(1024)(128)(4,1)}), s8[2097152]{0:T(1024)(128)(4,1)S(1)}, s32[]{:S(2)}) async-start(s8[6291456]{0:T(1024)(128)(4,1)} %bitcast.301), calls=%async_computation.12 | async-start | bytes 4194304
  249.9 84.6 %reduce-scatter.5.cloned.1.call-start = ((), (), s32[]{:S(2)}) async-start(), calls=%async_computation.9 | async-start | bytes 2359296 | tf_op jit(solution)/shard_map/reduce_scatter | solution.py:179
  261.9 198.6 %all-reduce.8.cloned.1.call-start = ((), (), s32[]{:S(2)}) async-start(), calls=%async_computation.5 | async-start | bytes 6291456 | tf_op jit(solution)/shard_map/psum | solution.py:172
  265.8 24.4 %copy-start.19 = (bf16[3072,256]{1,0:T(8,128)(2,1)S(1)}, bf16[3072,256]{1,0:T(8,128)(2,1)}, u32[]{:S(2)}) copy-start(bf16[3072,256]{1,0:T(8,128)(2,1)} %param.21) | copy-start | bytes 4718596
  294.5 44.8 %copy-start.36 = (s32[6]{0:T(128)S(1)}, s32[6]{0:T(128)}, u32[]{:S(2)}) copy-start(s32[6]{0:T(128)} %param.30) | copy-start | bytes 76
  294.5 44.8 %copy-start.32 = (f32[6,256]{1,0:T(8,128)S(1)}, f32[6,256]{1,0:T(8,128)}, u32[]{:S(2)}) copy-start(f32[6,256]{1,0:T(8,128)} %param.29) | copy-start | bytes 18436
  294.5 47.6 %copy-start.25 = (bf16[256,768]{1,0:T(8,128)(2,1)S(1)}, bf16[256,768]{1,0:T(8,128)(2,1)}, u32[]{:S(2)}) copy-start(bf16[256,768]{1,0:T(8,128)(2,1)} %param.28) | copy-start | bytes 1179652
  339.3 156.7 %all-gather.10.cloned.1.call-start = ((), (), s32[]{:S(2)}) async-start(), calls=%async_computation.6 | async-start | bytes 3538944 | tf_op jit(solution)/shard_map/all_gather | solution.py:14
  342.9 8.0 %copy-start.17 = (bf16[2,128,6,128]{3,1,0,2:T(8,128)(2,1)}, bf16[2,128,6,128]{3,1,0,2:T(8,128)(2,1)S(1)}, u32[]{:S(2)}) copy-start(bf16[2,128,6,128]{3,1,0,2:T(8,128)(2,1)S(1)} %copy.168) | copy-start | bytes 1179652
  343.2 10.0 %copy-start.15 = (bf16[2,128,6,128]{1,0,3,2:T(2,128)(2,1)}, bf16[2,128,6,128]{1,0,3,2:T(2,128)(2,1)S(1)}, u32[]{:S(2)}) copy-start(bf16[2,128,6,128]{1,0,3,2:T(2,128)(2,1)S(1)} %reshape.160) | copy-start | bytes 1179652
  347.7 254.4 %all-reduce.10.cloned.1.call-start = ((), (), s32[]{:S(2)}) async-start(), calls=%async_computation.10 | async-start | bytes 12582912 | tf_op jit(solution)/shard_map/psum | solution.py:249
  353.2 283.1 %all-gather.12.cloned.1.call-start = ((), (), s32[]{:S(2)}) async-start(), calls=%async_computation.7 | async-start | bytes 3538944 | tf_op jit(solution)/shard_map/all_gather | solution.py:14
  354.5 110.0 %copy-start.16 = (bf16[2,128,6,128]{1,0,3,2:T(2,128)(2,1)}, bf16[2,128,6,128]{1,0,3,2:T(2,128)(2,1)S(1)}, u32[]{:S(2)}) copy-start(bf16[2,128,6,128]{1,0,3,2:T(2,128)(2,1)S(1)} %reshape.162) | copy-start | bytes 1179652
  354.9 115.3 %copy-start.9 = (bf16[2,128,6,128]{3,1,2,0:T(8,128)(2,1)}, bf16[2,128,6,128]{3,1,2,0:T(8,128)(2,1)S(1)}, u32[]{:S(2)}) copy-start(bf16[2,128,6,128]{3,1,2,0:T(8,128)(2,1)S(1)} %copy.186) | copy-start | bytes 1179652
  612.7 37.8 %copy-start.34 = (f32[6]{0:T(128)S(1)}, f32[6]{0:T(128)}, u32[]{:S(2)}) copy-start(f32[6]{0:T(128)} %copy-done.33) | copy-start | bytes 76
  636.3 16.9 %copy-start.10 = (bf16[2,128,6,128]{3,1,2,0:T(8,128)(2,1)S(1)}, bf16[2,128,6,128]{3,1,2,0:T(8,128)(2,1)}, u32[]{:S(2)}) copy-start(bf16[2,128,6,128]{3,1,2,0:T(8,128)(2,1)} %copy-done.9) | copy-start | bytes 1179652
  (24 other events, 77.2 us)
Sparse Core Ops, SparseCore 0:
  11.4 26.1 all-gather.7
  40.0 23.3 all-gather.5
  106.2 121.0 all-reduce.5
  250.1 40.1 reduce-scatter.2
  293.4 41.1 reduce-scatter.4
  339.4 121.0 all-reduce.7
  463.0 31.3 all-gather.9
  498.2 103.8 all-reduce.9
  604.0 32.2 all-gather.11
where the time goes:
time: 668 us; the launch traced here: 662 us
  waiting for transfers between devices  402 us (60%)
  matrix products  125 us (19%)
  local copies, waits for them, and re-layouts  56 us (8%)
  other arithmetic  48.8 us (7%)
  between operations  15.5 us (2%)
  blocking collectives  14.7 us (2%)
    psum x2, waiting for transfers between devices, head_total(): summed = lax.psum(partial_value, 'head')  203 us
    psum x1, waiting for transfers between devices, local(): lax.psum((key_weight_part, value_weight_part), 'seq')  86 us
    reduce_scatter x1, waiting for transfers between devices, reduce_keys(): lax.psum_scatter(value_part, 'seq', scatter_dimension=0, tiled=True)  40 us
    dot_general x7, matrix products, contract_last(): lax.dot_general(left, right, (((1,), (1,)), ((), ())), preferred_element_...  34.4 us
    all_gather x2, waiting for transfers between devices, carried_in(): everything = jax.tree.map(lambda part: lax.all_gather(part, axis), value)  22 us
    unnamed x91, local copies, waits for them, and re-layouts  21.9 us
    all_gather x1, waiting for transfers between devices, local(): lax.all_gather(keys_own, 'seq', axis=0, tiled=True)  20.8 us
    sub x2, matrix products, attend_back(): raised = jnp.exp(scores - top)  19.6 us
  transfers between devices with their start and end apart: 9, of which 8 were waited for; matrix products, arithmetic and copies ran while one was open for 20% of the time, Pallas kernels for 0%

commit v1 on v0

--- a/solution.py
+++ b/solution.py
@@ -169,7 +169,10 @@
 
 
 def head_total(partial_value, residual):
-    summed = lax.psum(partial_value, "head")
+    devices, summed = (lax.axis_size("head"), partial_value)
+    for hop in [1 << k_2 for k_2 in range(devices.bit_length() - 1)]:
+        swap = [(i, i ^ hop) for i in range(devices)]
+        summed = summed + lax.ppermute(summed, "head", swap)
     return (residual.astype(jnp.float32) + summed).astype(jnp.bfloat16)
 
 

time: 668 us -> 741 us (1.11)
  waiting for transfers between devices: 402 us -> 456 us
  local copies, waits for them, and re-layouts: 56 us -> 64.6 us
  matrix products: 125 us -> 117 us
  starting transfers between devices: 1.01 us -> 8.49 us
    ppermute x0 -> x4, waiting for transfers between devices: none -> 375 us  [head_total(): summed = summed + lax.ppermute(summed, 'head', swap)]
    psum x2 -> x0, waiting for transfers between devices: 203 us -> none  [head_total(): summed = lax.psum(partial_value, 'head')]
    psum x1, waiting for transfers between devices: 86 us -> 0.01 us  [local(): lax.psum((key_weight_part, value_weight_part), 'seq')]
    all_gather x2, waiting for transfers between devices: 22 us -> 0.01 us  [carried_in(): everything = jax.tree.map(lambda part: lax.all_gather(part, axis), value)]
    reduce_scatter x1, waiting for transfers between devices: 18.9 us -> 7.27 us  [reduce_keys(): lax.psum_scatter(key_part, 'seq', scatter_dimension=0, tiled=True)]
    ppermute x0 -> x4, starting transfers between devices: none -> 7.95 us  [head_total(): summed = summed + lax.ppermute(summed, 'head', swap)]
    unnamed x91 -> x101, local copies, waits for them, and re-layouts: 21.9 us -> 24.6 us
  transfers between devices with their start and end apart: 9 -> 11, of which waited for: 8 -> 8; matrix products, arithmetic and copies ran while one was open for 20% -> 19% of each run, Pallas kernels for 0% -> 0%
where the time goes in v1:
time: 741 us; the launch traced here: 731 us
  waiting for transfers between devices  456 us (62%)
  matrix products  117 us (16%)
  local copies, waits for them, and re-layouts  64.6 us (9%)
  other arithmetic  55.5 us (7%)
  between operations  16 us (2%)
  blocking collectives  13.3 us (2%)
  starting transfers between devices  8.49 us (1%)
    ppermute x4, waiting for transfers between devices, head_total(): summed = summed + lax.ppermute(summed, 'head', swap)  375 us
    reduce_scatter x1, waiting for transfers between devices, reduce_keys(): lax.psum_scatter(value_part, 'seq', scatter_dimension=0, tiled=True)  40 us
    dot_general x7, matrix products, contract_last(): lax.dot_general(left, right, (((1,), (1,)), ((), ())), preferred_element_...  29.8 us
    unnamed x101, local copies, waits for them, and re-layouts  24.6 us
    all_gather x1, waiting for transfers between devices, local(): lax.all_gather(keys_own, 'seq', axis=0, tiled=True)  21.2 us
    sub x2, matrix products, attend_back(): raised = jnp.exp(scores - top)  19.7 us
    select_n x16, other arithmetic, lap(): return jax.tree.map(lambda a, b: jnp.where(reached, a, b), new, before)  17.8 us
    convert_element_type x2, other arithmetic, attend_back(): rounded = probs.astype(jnp.bfloat16)  16.6 us
  transfers between devices with their start and end apart: 11, of which 8 were waited for; matrix products, arithmetic and copies ran while one was open for 19% of the time, Pallas kernels for 0%

profile of v1, /device:TPU:0, one launch (start us, length us, event | category | flops | bytes accessed | tf_op | source)
XLA Modules:
  0.0 730.8 jit_solution(14714444197125903966)
XLA Ops:
  12.6 4.3 fusion.59
  17.9 4.5 fusion.62
  25.0 12.5 %all-gather.8.cloned.1.call-done = bf16[2048,256]{1,0:T(8,128)(2,1)} async-done(((bf16[256,256]{1,0:T(8,128)(2,1)}), bf16[2048,256]{1,0:T(8,128)(2,1)}) %all-gather.8.cloned.1.call-update) | async-done | bytes 1048592 | tf_op jit(solution)/shard_map/all_gather | solution.py:221
  42.1 21.2 %all-gather.6.cloned.1.call-done = bf16[2048,256]{1,0:T(8,128)(2,1)} async-done(((bf16[256,256]{1,0:T(8,128)(2,1)}), bf16[2048,256]{1,0:T(8,128)(2,1)}) %all-gather.6.cloned.1.call-update) | async-done | bytes 1048592 | tf_op jit(solution)/shard_map/all_gather | solution.py:220
  69.2 9.8 %fusion.131 = (f32[2,3,256]{2,1,0:T(4,128)S(1)}, f32[2,3,256,2048]{2,3,1,0:T(8,128)}) fusion(pred[256,2048]{0,1:T(8,128)(4,1)} %fusion.44, bf16[256,2,3,128]{0,3,2,1:T(8,128)(2,1)S(1)} %bitcast.322, bf16[2048,2,128,1]{2,1,0,3:T(2,128)(2,1)} %bitcast.309), kind=kOutput, calls=%fused_computation.175 | convolution fusion | flops 817891328 | bytes 14555136 | tf_op jit(solution)/shard_map/sub | solution.py:54
  79.0 8.2 %fusion.18 = bf16[2,3,256,2048]{2,3,1,0:T(8,128)(2,1)} fusion(f32[2,3,256,2048]{2,3,1,0:T(8,128)} %get-tuple-element.351, f32[2,3,256]{2,1,0:T(4,128)S(1)} %get-tuple-element.350), kind=kLoop, calls=%fused_computation.30 | loop fusion | flops 6291456 | bytes 18880512 | tf_op jit(solution)/shard_map/convert_element_type | solution.py:56
  91.1 6.0 fusion.9
  105.2 68.8 %collective-permute-done = f32[256,3072]{1,0:T(8,128)S(1)} collective-permute-done((f32[256,3072]{1,0:T(8,128)S(1)}, f32[256,3072]{1,0:T(8,128)S(1)}, u32[]{:S(2)}, u32[]{:S(2)}) %collective-permute-start) | collective-permute-done | bytes 3145760 | tf_op jit(solution)/shard_map/ppermute | solution.py:175
  181.9 9.9 %fusion.126 = (f32[2,3,256]{2,1,0:T(4,128)S(1)}, f32[2,3,256,2048]{2,3,1,0:T(8,128)}) fusion(pred[256,2048]{0,1:T(8,128)(4,1)} %fusion.44, bf16[256,2,3,128]{0,3,2,1:T(8,128)(2,1)S(1)} %bitcast.320, bf16[2048,2,128,1]{2,1,0,3:T(2,128)(2,1)} %bitcast.310), kind=kOutput, calls=%fused_computation.174 | convolution fusion | flops 817891328 | bytes 14555136 | tf_op jit(solution)/shard_map/sub | solution.py:54
  191.8 8.4 %fusion.19 = bf16[2,3,256,2048]{2,3,1,0:T(8,128)(2,1)} fusion(f32[2,3,256,2048]{2,3,1,0:T(8,128)} %get-tuple-element.349, f32[2,3,256]{2,1,0:T(4,128)S(1)} %get-tuple-element.348), kind=kLoop, calls=%fused_computation.31 | loop fusion | flops 6291456 | bytes 18880512 | tf_op jit(solution)/shard_map/convert_element_type | solution.py:56
  200.2 114.0 %collective-permute-done.1 = f32[256,3072]{1,0:T(8,128)} collective-permute-done((f32[256,3072]{1,0:T(8,128)}, f32[256,3072]{1,0:T(8,128)}, u32[]{:S(2)}, u32[]{:S(2)}) %collective-permute-start.1) | collective-permute-done | bytes 3145760 | tf_op jit(solution)/shard_map/ppermute | solution.py:175
  318.9 4.5 fusion.68
  328.9 5.9 fusion.6
  341.0 4.9 convolution_bitcast_fusion.2
  346.0 6.5 fusion.43
  369.3 5.6 fusion.22
  375.0 7.3 reduce-scatter.3.cloned.1.call-done
  382.2 4.3 convolution_add_fusion.1
  386.5 40.0 %reduce-scatter.5.cloned.1.call-done = f32[256,256]{0,1:T(8,128)} async-done(((f32[2048,256]{0,1:T(8,128)}), f32[256,256]{0,1:T(8,128)}) %reduce-scatter.5.cloned.1.call-update) | async-done | bytes 262160 | tf_op jit(solution)/shard_map/reduce_scatter | solution.py:182
  431.2 68.2 %collective-permute-done.2 = f32[256,3072]{1,0:T(8,128)S(1)} collective-permute-done((f32[256,3072]{1,0:T(8,128)S(1)}, f32[256,3072]{1,0:T(8,128)S(1)}, u32[]{:S(2)}, u32[]{:S(2)}) %collective-permute-start.2) | collective-permute-done | bytes 3145760 | tf_op jit(solution)/shard_map/ppermute | solution.py:175
  515.1 123.8 %collective-permute-done.3 = f32[256,3072]{1,0:T(8,128)} collective-permute-done((f32[256,3072]{1,0:T(8,128)}, f32[256,3072]{1,0:T(8,128)}, u32[]{:S(2)}, u32[]{:S(2)}) %collective-permute-start.3) | collective-permute-done | bytes 3145760 | tf_op jit(solution)/shard_map/ppermute | solution.py:175
  654.4 13.3 %all-reduce = f32[48]{0:T(128)} all-reduce(f32[48]{0:T(128)} %dynamic-update-slice), channel_id=2, replica_groups=mesh['seq'=8,'head'=4] {'seq'}, use_global_device_ids=true, to_apply=%add | all-reduce | flops 48 | bytes 384
  671.9 18.2 %while.30 = (s32[]{:T(128)}, f32[6,128,128]{2,1,0:T(8,128)S(1)}, s32[]{:T(128)}, f32[8,6,1,1]{1,3,2,0:T(1,128)}, f32[8,6,128,128]{3,2,1,0:T(8,128)}, /*index=5*/s32[]{:T(128)}, s32[]{:T(128)}) while((s32[]{:T(128)}, f32[6,128,128]{2,1,0:T(8,128)S(1)}, s32[]{:T(128)}, f32[8,6,1,1]{1,3,2,0:T(1,128)}, ...), condition=%wide.region_13.14_spmd.clone, body=%wide.region_12.13_spmd.clone.sunk | while | flops 393220 | bytes 1179825 | solution.py:27
  704.1 14.2 %while.31 = (s32[]{:T(128)}, f32[6,128,128]{2,1,0:T(8,128)S(1)}, s32[]{:T(128)}, f32[8,6,128,128]{3,2,1,0:T(8,128)}, f32[8,6,1,1]{1,3,2,0:T(1,128)}, /*index=5*/s32[]{:T(128)}, s32[]{:T(128)}, s32[]{:T(128)}, s32[]{:T(128)}) while((s32[]{:T(128)}, f32[6,128,128]{2,1,0:T(8,128)S(1)}, s32[]{:T(128)}, ...), condition=%wide.region_15.16_spmd.clone, body=%wide.region_14.15_spmd.clone.sunk | while | flops 393224 | bytes 1179887 | solution.py:27
  (225 shorter events, 162.5 us)
Async XLA Ops:
  7.2 30.3 %all-gather.8.cloned.1.call-start = ((), (), s32[]{:S(2)}) async-start(), calls=%async_computation.3 | async-start | bytes 1179648 | tf_op jit(solution)/shard_map/all_gather | solution.py:221
  11.2 52.1 %all-gather.6.cloned.1.call-start = ((), (), s32[]{:S(2)}) async-start(), calls=%async_computation.2 | async-start | bytes 1179648 | tf_op jit(solution)/shard_map/all_gather | solution.py:220
  12.5 369.7 %reduce-scatter.3.cloned.1.call-start = ((), (), s32[]{:S(2)}) async-start(), calls=%async_computation.6 | async-start | bytes 2359296 | tf_op jit(solution)/shard_map/reduce_scatter | solution.py:181
  39.6 29.6 %copy-start.24 = (bf16[256,768]{0,1:T(8,128)(2,1)S(1)}, bf16[256,768]{0,1:T(8,128)(2,1)}, u32[]{:S(2)}) copy-start(bf16[256,768]{0,1:T(8,128)(2,1)} %copy.141) | copy-start | bytes 1179652
  99.8 78.8 %slice-start.2 = ((s8[9437184]{0:T(1024)(128)(4,1)}), s8[4194304]{0:T(1024)(128)(4,1)S(1)}, s32[]{:S(2)}) async-start(s8[9437184]{0:T(1024)(128)(4,1)} %bitcast.331), calls=%async_computation.11 | async-start | bytes 8388608
  99.8 78.8 %slice-start.3 = ((s8[9437184]{0:T(1024)(128)(4,1)}), s8[4194304]{0:T(1024)(128)(4,1)S(1)}, s32[]{:S(2)}) async-start(s8[9437184]{0:T(1024)(128)(4,1)} %bitcast.331), calls=%async_computation.12 | async-start | bytes 8388608
  103.7 74.9 %slice-start.4 = ((s8[9437184]{0:T(1024)(128)(4,1)}), s8[1048576]{0:T(1024)(128)(4,1)S(1)}, s32[]{:S(2)}) async-start(s8[9437184]{0:T(1024)(128)(4,1)} %bitcast.331), calls=%async_computation.13 | async-start | bytes 2097152
  103.7 70.3 %collective-permute-start = (f32[256,3072]{1,0:T(8,128)S(1)}, f32[256,3072]{1,0:T(8,128)S(1)}, u32[]{:S(2)}, u32[]{:S(2)}) collective-permute-start(f32[256,3072]{1,0:T(8,128)S(1)} %fusion.28), channel_id=1, source_target_pairs={{0,1},{1,0},{2,3},{3,2},{4,5},{5,4},{6,7},{7,6},{8,9},{9,8},{10,11... | collective-permute-start | bytes 9437192 | tf_op jit(solution)/shard_map/ppermute | solution.py:175
  176.2 138.0 %collective-permute-start.1 = (f32[256,3072]{1,0:T(8,128)}, f32[256,3072]{1,0:T(8,128)}, u32[]{:S(2)}, u32[]{:S(2)}) collective-permute-start(f32[256,3072]{1,0:T(8,128)} %add.179), channel_id=1, source_target_pairs={{0,2},{1,3},{2,0},{3,1},{4,6},{5,7},{6,4},{7,5},{8,10},{9,11},{10,... | collective-permute-start | bytes 9437192 | tf_op jit(solution)/shard_map/ppermute | solution.py:175
  181.9 9.9 %copy-start.14 = (bf16[256,768]{0,1:T(8,128)(2,1)}, bf16[256,768]{0,1:T(8,128)(2,1)S(1)}, u32[]{:S(2)}) copy-start(bf16[256,768]{0,1:T(8,128)(2,1)S(1)} %copy.151) | copy-start | bytes 1179652
  191.8 122.4 %copy-start.17 = (bf16[256,3072]{1,0:T(8,128)(2,1)S(1)}, bf16[256,3072]{1,0:T(8,128)(2,1)}, u32[]{:S(2)}) copy-start(bf16[256,3072]{1,0:T(8,128)(2,1)} %param.20) | copy-start | bytes 4718596
  324.7 12.8 %slice-start = ((s8[6291456]{0:T(1024)(128)(4,1)}), s8[4194304]{0:T(1024)(128)(4,1)S(1)}, s32[]{:S(2)}) async-start(s8[6291456]{0:T(1024)(128)(4,1)} %bitcast.298), calls=%async_computation.9 | async-start | bytes 8388608
  341.0 85.5 %reduce-scatter.5.cloned.1.call-start = ((), (), s32[]{:S(2)}) async-start(), calls=%async_computation.7 | async-start | bytes 2359296 | tf_op jit(solution)/shard_map/reduce_scatter | solution.py:182
  352.5 319.4 %all-gather.10.cloned.1.call-start = ((), (), s32[]{:S(2)}) async-start(), calls=%async_computation.4 | async-start | bytes 3538944 | tf_op jit(solution)/shard_map/all_gather | solution.py:14
  355.7 9.7 %copy-start.4 = (bf16[2048,2,128,1]{0,2,3,1:T(8,128)(2,1)S(1)}, bf16[2048,2,128,1]{0,2,3,1:T(8,128)(2,1)}, u32[]{:S(2)}) copy-start(bf16[2048,2,128,1]{0,2,3,1:T(8,128)(2,1)} %copy.216) | copy-start | bytes 3145732
  365.1 326.8 %all-reduce.4.cloned.1.call-start = ((), (), s32[]{:S(2)}) async-start(), calls=%async_computation.8 | async-start | bytes 12582912 | tf_op jit(solution)/shard_map/psum | solution.py:252
  369.3 12.9 %copy-start.21 = (bf16[3072,256]{1,0:T(8,128)(2,1)S(1)}, bf16[3072,256]{1,0:T(8,128)(2,1)}, u32[]{:S(2)}) copy-start(bf16[3072,256]{1,0:T(8,128)(2,1)} %param.21) | copy-start | bytes 4718596
  429.6 74.4 %copy-start.27 = (f32[256,256]{0,1:T(8,128)S(1)}, f32[256,256]{0,1:T(8,128)}, u32[]{:S(2)}) copy-start(f32[256,256]{0,1:T(8,128)} %reduce-scatter.5.cloned.1.call-done) | copy-start | bytes 786436
  429.6 69.7 %collective-permute-start.2 = (f32[256,3072]{1,0:T(8,128)S(1)}, f32[256,3072]{1,0:T(8,128)S(1)}, u32[]{:S(2)}, u32[]{:S(2)}) collective-permute-start(f32[256,3072]{1,0:T(8,128)S(1)} %convolution_add_fusion), channel_id=1, source_target_pairs={{0,1},{1,0},{2,3},{3,2},{4,5},{5,4},{6,7},{7,6},{8,9},{9,8},{10,11... | collective-permute-start | bytes 9437192 | tf_op jit(solution)/shard_map/ppermute | solution.py:175
  501.5 137.5 %collective-permute-start.3 = (f32[256,3072]{1,0:T(8,128)}, f32[256,3072]{1,0:T(8,128)}, u32[]{:S(2)}, u32[]{:S(2)}) collective-permute-start(f32[256,3072]{1,0:T(8,128)} %add.186), channel_id=1, source_target_pairs={{0,2},{1,3},{2,0},{3,1},{4,6},{5,7},{6,4},{7,5},{8,10},{9,11},{10,... | collective-permute-start | bytes 9437192 | tf_op jit(solution)/shard_map/ppermute | solution.py:175
  508.5 130.5 %copy-start.6 = (bf16[256,3072]{1,0:T(8,128)(2,1)S(1)}, bf16[256,3072]{1,0:T(8,128)(2,1)}, u32[]{:S(2)}) copy-start(bf16[256,3072]{1,0:T(8,128)(2,1)} %copy-done.5) | copy-start | bytes 4718596
  508.5 195.6 %all-gather.12.cloned.1.call-start = ((), (), s32[]{:S(2)}) async-start(), calls=%async_computation.5 | async-start | bytes 3538944 | tf_op jit(solution)/shard_map/all_gather | solution.py:14
  704.1 14.2 %copy-start.34 = (f32[6]{0:T(128)S(1)}, f32[6]{0:T(128)}, u32[]{:S(2)}) copy-start(f32[6]{0:T(128)} %copy-done.33) | copy-start | bytes 76
  704.1 15.4 %copy-start.12 = (bf16[2,128,6,128]{1,0,3,2:T(2,128)(2,1)S(1)}, bf16[2,128,6,128]{1,0,3,2:T(2,128)(2,1)}, u32[]{:S(2)}) copy-start(bf16[2,128,6,128]{1,0,3,2:T(2,128)(2,1)} %copy-done.11) | copy-start | bytes 1179652
  (31 other events, 120.6 us)
Sparse Core Ops, SparseCore 0:
  11.4 26.0 all-gather.7
  39.9 23.3 all-gather.5
  341.1 41.0 reduce-scatter.2
  385.4 41.1 reduce-scatter.4
  428.8 32.1 all-gather.9
  508.6 102.0 all-reduce.3
  650.8 32.1 all-gather.11
